TPU v7x, 32 devices: a whole 2x2x4 slice. The times are simulated.
32 devices in a mesh: front: 4 (over y, core), blk: 8 (over z, x).
Axes of the slice: x: 2, y: 2, z: 4, core: 2. Of those that a mesh axis runs over, the one named last changes fastest.
Arguments:
- front: float32 [4, 1024, 1024], P('front', 'blk'), parts along dimension 0, may hold values from -8 to 40, as said below
- child: float32 [4, 512, 512], P('front', 'blk'), parts along dimension 0, may hold values from -1 to 4, as said below
- index_map: int32 [2048], P('front'), parts along dimension 0, may hold values from 0 to 1023, as said below
Outputs:
- factored: float32 [4, 1024, 1024], P('front', 'blk'), parts along dimension 0
There are 4 independent parts, one for each index of `front`. A program takes and returns all parts, laid end to end along the dimension named above; each array names one. Nothing has to cross between parts.
Inputs may be any that keep to these rules, and one draw needn't show every extreme that they name: front is symmetric and positive definite. child is symmetric and positive semidefinite. `index_map`: tile t of the child (indices t * 64 to t * 64 + 63, with t = k * 8 + e and e < 8) maps in increasing order onto 64 different indices of the front's block column b = k * 8 + ((e + h) mod 8), where h is half of 8, that is onto indices b * 128 to b * 128 + 127; no two child indices share a front index.
All inputs are finite; a program needn't handle non-finite values.
Results may differ from a plain program's by a relative error of at most 0.0034.
Values may be sent and summed in bfloat16 or wider, within the bound.
No kernel may reach another device: no remote copies, remote signals or barrier semaphores. Data moves between devices by JAX's collectives and lax.ppermute only.
A program may use at most 128 MiB of HBM per device.

v0:
```python
import jax
import jax.numpy as jnp
from jax import lax
from jax.sharding import PartitionSpec as P

PANEL_WIDTH = 512
BLOCK_WIDTH = 128
COL_BLOCKS = 1
TILE_WIDTH = 64
HIGHEST = lax.Precision.HIGHEST


def from_behind(shard, axis, by):
    count = lax.axis_size(axis)
    return lax.ppermute(shard, axis, [(i, (i + by) % count) for i in range(count)])


def column_numbers(cycle_size, my_index):
    local_ids = jnp.arange(COL_BLOCKS * BLOCK_WIDTH, dtype=jnp.int32)
    return (
        local_ids // BLOCK_WIDTH * cycle_size + my_index
    ) * BLOCK_WIDTH + local_ids % BLOCK_WIDTH


def row_numbers(cycle_size):
    stored = jnp.arange(cycle_size * COL_BLOCKS * BLOCK_WIDTH, dtype=jnp.int32)
    holder = stored // (COL_BLOCKS * BLOCK_WIDTH)
    within = stored // BLOCK_WIDTH % COL_BLOCKS
    return (within * cycle_size + holder) * BLOCK_WIDTH + stored % BLOCK_WIDTH


def cycle_rows(matrix, cycle_size):
    height = matrix.shape[0]
    return (
        matrix.reshape(height, COL_BLOCKS, cycle_size, BLOCK_WIDTH)
        .transpose(0, 2, 1, 3)
        .reshape(height, -1)
    )


def natural_rows(matrix, cycle_size):
    height = matrix.shape[0]
    return (
        matrix.reshape(height, cycle_size, COL_BLOCKS, BLOCK_WIDTH)
        .transpose(0, 2, 1, 3)
        .reshape(height, -1)
    )


def panel_rows(matrix, row_start, cycle_size):
    first_owner = row_start // BLOCK_WIDTH
    owner_count = PANEL_WIDTH // BLOCK_WIDTH
    height = matrix.shape[0]
    blocks = matrix.reshape(height, cycle_size, COL_BLOCKS, BLOCK_WIDTH)
    return blocks[:, first_owner : first_owner + owner_count, 0, :].reshape(height, PANEL_WIDTH)


def ownership(row_start, my_index):
    first_owner = row_start // BLOCK_WIDTH
    owner_count = PANEL_WIDTH // BLOCK_WIDTH
    is_owner = (my_index >= first_owner) & (my_index < first_owner + owner_count)
    column_start = jnp.clip(my_index - first_owner, 0, owner_count - 1) * BLOCK_WIDTH
    return (is_owner, column_start)


def collect(stacked, row_start, my_index):
    is_owner, column_start = ownership(row_start, my_index)
    padded = jnp.zeros((stacked.shape[0], PANEL_WIDTH, PANEL_WIDTH), jnp.float32)
    padded = lax.dynamic_update_slice(
        padded, jnp.where(is_owner, stacked, 0.0), (0, column_start, 0)
    )
    result = lax.psum(padded, "blk")
    return result


def own_rows(diag_factor, panel_part, row_start, columns):
    solved = lax.linalg.triangular_solve(
        diag_factor, panel_part, left_side=False, lower=True, transpose_a=True
    )
    offsets = columns - row_start
    diag_rows = jnp.take(diag_factor, jnp.clip(offsets, 0, PANEL_WIDTH - 1), axis=0)
    inside = (offsets >= 0) & (offsets < PANEL_WIDTH)
    before = offsets < 0
    return jnp.where(inside[:, None], diag_rows, jnp.where(before[:, None], 0.0, solved))


def make_refresh(working, lowered, owned_panels):

    def refresh(received, offset):
        updated = working - lax.dot_general(
            lowered, received, (((1,), (1,)), ((), ())), preferred_element_type=jnp.float32
        )
        leading = updated
        for is_owner, column_start in owned_panels:
            factor_column = (
                lax.dynamic_slice_in_dim(received, column_start, BLOCK_WIDTH, 1)
                .astype(jnp.float32)
                .T
            )
            leading = jnp.where(is_owner, factor_column, leading)
        return jnp.concatenate([leading, updated[BLOCK_WIDTH:]], axis=0)

    return refresh


def assemble(front, child, index_map, cycle_size, my_index):
    half_cycle = cycle_size // 2
    arrived_tiles = from_behind(child, "blk", half_cycle)
    full_order = 2 * index_map.shape[0]
    tile_places = (index_map % BLOCK_WIDTH).reshape(COL_BLOCKS, cycle_size, TILE_WIDTH)
    places = jnp.arange(BLOCK_WIDTH, dtype=jnp.int32)
    row_table = (tile_places[..., None] == places).astype(jnp.float32)
    shaped = arrived_tiles.reshape(COL_BLOCKS, TILE_WIDTH, COL_BLOCKS, cycle_size, TILE_WIDTH)
    spread = jnp.einsum("acbei,beiq->acbeq", shaped, row_table, precision=HIGHEST)
    spread = jnp.roll(spread, half_cycle, axis=3).reshape(COL_BLOCKS, TILE_WIDTH, full_order)
    source = (my_index - half_cycle) % cycle_size
    own_places = lax.dynamic_index_in_dim(tile_places, source, axis=1, keepdims=False)
    column_table = (own_places[..., None] == places).astype(jnp.float32)
    placed = jnp.einsum("kcq,kcn->kqn", column_table, spread, precision=HIGHEST)
    return front + placed


def on_device(front, child, index_map):
    cycle_size = lax.axis_size("blk")
    my_index = lax.axis_index("blk")
    local_width = COL_BLOCKS * BLOCK_WIDTH
    assembled = assemble(front, child, index_map, cycle_size, my_index).reshape(local_width, -1)
    working = cycle_rows(assembled, cycle_size)
    columns = column_numbers(cycle_size, my_index)
    for row_start in (0, PANEL_WIDTH):
        panel_part = panel_rows(working, row_start, cycle_size)
        diag_block = collect(panel_part[None, :BLOCK_WIDTH], row_start, my_index)[0]
        lowered = own_rows(jnp.linalg.cholesky(diag_block), panel_part, row_start, columns).astype(
            jnp.bfloat16
        )
        refresh = make_refresh(working, lowered, (ownership(row_start, my_index),))
        working = refresh(lax.all_gather(lowered, "blk", axis=0, tiled=True), jnp.int32(0))
    trailing = columns >= 2 * PANEL_WIDTH
    leading_rows = row_numbers(cycle_size) < 2 * PANEL_WIDTH
    working = jnp.where(trailing[:, None] & leading_rows[None, :], 0.0, working)
    return natural_rows(working, cycle_size).reshape(COL_BLOCKS, BLOCK_WIDTH, -1)


def solution(mesh):
    placed = (P("front", "blk", None), P("front", "blk", None), P("front"))
    return jax.shard_map(
        on_device, mesh=mesh, in_specs=placed, out_specs=P("front", "blk", None), check_vma=False
    )
```

profile of v0, /device:TPU:0, one launch (start us, length us, event | category | flops | bytes accessed | tf_op | source)
XLA Modules:
  0.0 557.0 jit_solution(17881052555522516391)
XLA Ops:
  6.5 4.1 collective-permute-start
  11.5 5.7 %collective-permute-done = f32[1,64,512]{2,1,0:T(8,128)S(1)} collective-permute-done((f32[1,64,512]{2,1,0:T(8,128)}, f32[1,64,512]{2,1,0:T(8,128)S(1)}, u32[]{:S(2)}, u32[]{:S(2)}) %collective-permute-start) | collective-permute-done | bytes 131104 | tf_op jit(solution)/shard_map/ppermute | solution.py:15
  17.8 0.8 copy-done.10
  19.6 1.0 copy-done.2
  20.7 79.5 %all-reduce.4.cloned.1.call-done = f32[512,512]{0,1:T(8,128)} async-done(((f32[512,512]{0,1:T(8,128)}), f32[512,512]{0,1:T(8,128)}) %all-reduce.4.cloned.1.call-update) | async-done | bytes 1048592 | tf_op jit(solution)/shard_map/psum | solution.py:72
  100.2 1.6 copy.13
  102.1 1.0 copy-done.6
  103.1 11.7 %cholesky.286 = f32[128,128]{1,0:T(8,128)S(1)} custom-call(f32[128,128]{1,0:T(8,128)S(1)} %cholesky.426), custom_call_target="Cholesky" | custom-call | tf_op jit(solution)/shard_map/jit(cholesky)/cholesky | solution.py:133
  115.0 9.8 %custom-call.27 = f32[1,128,128]{1,2,0:T(8,128)S(1)} custom-call(f32[1,128,128]{2,1,0:T(8,128)S(1)} %get-tuple-element.73), custom_call_target="InvertDiagBlocksLowerTriangular" | custom-call | tf_op jit(solution)/shard_map/jit(cholesky)/cholesky | solution.py:133
  125.5 11.7 %cholesky.305 = f32[128,128]{1,0:T(8,128)S(1)} custom-call(f32[128,128]{1,0:T(8,128)S(1)} %cholesky.430), custom_call_target="Cholesky" | custom-call | tf_op jit(solution)/shard_map/jit(cholesky)/cholesky | solution.py:133
  137.2 10.0 %custom-call.28 = f32[1,128,128]{1,2,0:T(8,128)S(1)} custom-call(f32[1,128,128]{2,1,0:T(8,128)S(1)} %get-tuple-element.70), custom_call_target="InvertDiagBlocksLowerTriangular" | custom-call | tf_op jit(solution)/shard_map/jit(cholesky)/cholesky | solution.py:133
  148.0 11.7 %cholesky.326 = f32[128,128]{1,0:T(8,128)S(1)} custom-call(f32[128,128]{1,0:T(8,128)S(1)} %cholesky.435), custom_call_target="Cholesky" | custom-call | tf_op jit(solution)/shard_map/jit(cholesky)/cholesky | solution.py:133
  159.7 0.7 compare_reduce_fusion.5
  160.4 9.8 %custom-call.29 = f32[1,128,128]{1,2,0:T(8,128)S(1)} custom-call(f32[1,128,128]{2,1,0:T(8,128)S(1)} %get-tuple-element.67), custom_call_target="InvertDiagBlocksLowerTriangular" | custom-call | tf_op jit(solution)/shard_map/jit(cholesky)/cholesky | solution.py:133
  170.8 11.7 %cholesky.343 = f32[128,128]{1,0:T(8,128)S(1)} custom-call(f32[128,128]{1,0:T(8,128)S(1)} %convolution_subtract_fusion.13), custom_call_target="Cholesky" | custom-call | tf_op jit(solution)/shard_map/jit(cholesky)/cholesky | solution.py:133
  186.5 12.0 %fusion.8 = (f32[512,512]{1,0:T(8,128)S(1)}, bf16[512,512]{1,0:T(8,128)(2,1)S(1)}) fusion(f32[512,512]{1,0:T(8,128)S(1)} %get-tuple-element.65, pred[]{:T(512)S(6)} %cholesky.348), kind=kLoop, calls=%fused_computation.38 | loop fusion | flops 1310720 | bytes 2621441 | tf_op jit(solution)/shard_map/triangular_solve/select.3 | solution.py:77
  198.5 8.1 %while.4 = (s32[]{:T(128)}, f32[512,512]{1,0:T(8,128)S(1)}, s32[4,2]{0,1:T(2,128)S(1)}, f32[4,128,128]{2,1,0:T(8,128)S(1)}, s32[]{:T(128)}) while((s32[]{:T(128)}, f32[512,512]{1,0:T(8,128)S(1)}, s32[4,2]{0,1:T(2,128)S(1)}, f32[4,128,128]{2,1,0:T(8,128)S(1)}, s32[]{:T(128)}) %tuple.61), condition=%wide.while_cond, body=%wide.while_body.sunk | while | flops 2 | bytes 131181 | solution.py:77
  199.1 1.3 bitcast_dynamic-update-slice_fusion.4
  201.2 1.3 bitcast_dynamic-update-slice_fusion.4
  203.2 1.3 bitcast_dynamic-update-slice_fusion.4
  205.3 1.3 bitcast_dynamic-update-slice_fusion.4
  206.6 39.3 %custom-call.30 = f32[4,128,128]{1,2,0:T(8,128)S(1)} custom-call(f32[4,128,128]{2,1,0:T(8,128)S(1)} %get-tuple-element.22), custom_call_target="InvertDiagBlocksLowerTriangular" | custom-call | tf_op jit(solution)/shard_map/triangular_solve/custom-call.3 | solution.py:77
  247.9 0.8 gather_fusion
  248.9 0.7 fusion.15
  249.7 39.1 %all-gather.3.cloned.1.call-done = bf16[1024,512]{0,1:T(8,128)(2,1)} async-done(((bf16[128,512]{0,1:T(8,128)(2,1)}), bf16[1024,512]{0,1:T(8,128)(2,1)}) %all-gather.3.cloned.1.call-update) | async-done | bytes 1048592 | tf_op jit(solution)/shard_map/all_gather | solution.py:137
  288.8 1.6 fusion
  290.8 1.0 copy-done.3
  292.0 77.6 %all-reduce.6.cloned.1.call-done = f32[512,512]{0,1:T(8,128)} async-done(((f32[512,512]{0,1:T(8,128)}), f32[512,512]{0,1:T(8,128)}) %all-reduce.6.cloned.1.call-update) | async-done | bytes 1048592 | tf_op jit(solution)/shard_map/psum | solution.py:72
  369.6 1.6 copy.16
  371.5 1.0 copy-done.4
  372.5 11.7 %cholesky.358 = f32[128,128]{1,0:T(8,128)S(1)} custom-call(f32[128,128]{1,0:T(8,128)S(1)} %cholesky.439), custom_call_target="Cholesky" | custom-call | tf_op jit(solution)/shard_map/jit(cholesky)/cholesky | solution.py:133
  384.4 9.8 %custom-call.31 = f32[1,128,128]{1,2,0:T(8,128)S(1)} custom-call(f32[1,128,128]{2,1,0:T(8,128)S(1)} %get-tuple-element.63), custom_call_target="InvertDiagBlocksLowerTriangular" | custom-call | tf_op jit(solution)/shard_map/jit(cholesky)/cholesky | solution.py:133
  394.9 11.7 %cholesky.377 = f32[128,128]{1,0:T(8,128)S(1)} custom-call(f32[128,128]{1,0:T(8,128)S(1)} %cholesky.443), custom_call_target="Cholesky" | custom-call | tf_op jit(solution)/shard_map/jit(cholesky)/cholesky | solution.py:133
  406.6 0.7 compare_reduce_fusion.2
  408.0 10.0 %custom-call.32 = f32[1,128,128]{1,2,0:T(8,128)S(1)} custom-call(f32[1,128,128]{2,1,0:T(8,128)S(1)} %get-tuple-element.60), custom_call_target="InvertDiagBlocksLowerTriangular" | custom-call | tf_op jit(solution)/shard_map/jit(cholesky)/cholesky | solution.py:133
  418.7 11.7 %cholesky.398 = f32[128,128]{1,0:T(8,128)S(1)} custom-call(f32[128,128]{1,0:T(8,128)S(1)} %cholesky.448), custom_call_target="Cholesky" | custom-call | tf_op jit(solution)/shard_map/jit(cholesky)/cholesky | solution.py:133
  431.0 9.8 %custom-call.33 = f32[1,128,128]{1,2,0:T(8,128)S(1)} custom-call(f32[1,128,128]{2,1,0:T(8,128)S(1)} %get-tuple-element.57), custom_call_target="InvertDiagBlocksLowerTriangular" | custom-call | tf_op jit(solution)/shard_map/jit(cholesky)/cholesky | solution.py:133
  441.5 11.7 %cholesky.415 = f32[128,128]{1,0:T(8,128)S(1)} custom-call(f32[128,128]{1,0:T(8,128)S(1)} %convolution_subtract_fusion.11), custom_call_target="Cholesky" | custom-call | tf_op jit(solution)/shard_map/jit(cholesky)/cholesky | solution.py:133
  456.9 8.5 %while.5 = (s32[]{:T(128)}, f32[512,512]{1,0:T(8,128)S(1)}, s32[4,2]{0,1:T(2,128)S(1)}, f32[4,128,128]{2,1,0:T(8,128)S(1)}, s32[]{:T(128)}) while((s32[]{:T(128)}, f32[512,512]{1,0:T(8,128)S(1)}, s32[4,2]{0,1:T(2,128)S(1)}, f32[4,128,128]{2,1,0:T(8,128)S(1)}, s32[]{:T(128)}) %tuple.75), condition=%wide.while_cond.clone, body=%wide.while_body.clone.sunk | while | flops 2 | bytes 131181 | solution.py:77
  457.5 1.4 bitcast_dynamic-update-slice_fusion.5
  459.7 1.4 bitcast_dynamic-update-slice_fusion.5
  461.8 1.4 bitcast_dynamic-update-slice_fusion.5
  463.9 1.4 bitcast_dynamic-update-slice_fusion.5
  465.4 39.3 %custom-call.34 = f32[4,128,128]{1,2,0:T(8,128)S(1)} custom-call(f32[4,128,128]{2,1,0:T(8,128)S(1)} %get-tuple-element.23), custom_call_target="InvertDiagBlocksLowerTriangular" | custom-call | tf_op jit(solution)/shard_map/triangular_solve/custom-call.3 | solution.py:77
  506.7 0.8 gather_fusion.1
  507.7 0.7 fusion.17
  508.4 39.1 %all-gather.5.cloned.1.call-done = bf16[1024,512]{0,1:T(8,128)(2,1)} async-done(((bf16[128,512]{0,1:T(8,128)(2,1)}), bf16[1024,512]{0,1:T(8,128)(2,1)}) %all-gather.5.cloned.1.call-update) | async-done | bytes 1048592 | tf_op jit(solution)/shard_map/all_gather | solution.py:137
  547.6 2.4 fusion.3
  (125 shorter events, 20.9 us)
Async XLA Ops:
  6.5 93.7 %all-reduce.4.cloned.1.call-start = ((), (), s32[]{:S(2)}) async-start(), calls=%async_computation | async-start | bytes 2097152 | tf_op jit(solution)/shard_map/psum | solution.py:72
  6.5 10.6 %collective-permute-start = (f32[1,64,512]{2,1,0:T(8,128)}, f32[1,64,512]{2,1,0:T(8,128)S(1)}, u32[]{:S(2)}, u32[]{:S(2)}) collective-permute-start(f32[1,64,512]{2,1,0:T(8,128)} %param.9), channel_id=1, source_target_pairs={{0,4},{1,5},{2,6},{3,7},{4,0},{5,1},{6,2},{7,3},{8,12},{9,13},{10,... | collective-permute-start | bytes 393224 | tf_op jit(solution)/shard_map/ppermute | solution.py:15
  17.6 1.0 copy-start.10
  19.6 1.0 copy-start.2
  20.6 268.2 %all-gather.3.cloned.1.call-start = ((), (), s32[]{:S(2)}) async-start(), calls=%async_computation.1 | async-start | bytes 1179648 | tf_op jit(solution)/shard_map/all_gather | solution.py:137
  100.2 1.7 copy-start
  102.1 1.0 copy-start.6
  103.1 21.7 %copy-start.7 = (f32[512,512]{1,0:T(8,128)S(1)}, f32[512,512]{1,0:T(8,128)}, u32[]{:S(2)}) copy-start(f32[512,512]{1,0:T(8,128)} %copy-done.6) | copy-start | bytes 3145732
  249.6 39.2 %copy-start.8 = (bf16[128,512]{0,1:T(8,128)(2,1)S(1)}, bf16[128,512]{0,1:T(8,128)(2,1)}, u32[]{:S(2)}) copy-start(bf16[128,512]{0,1:T(8,128)(2,1)} %fusion.15) | copy-start | bytes 393220
  249.7 119.9 %all-reduce.6.cloned.1.call-start = ((), (), s32[]{:S(2)}) async-start(), calls=%async_computation.2 | async-start | bytes 2097152 | tf_op jit(solution)/shard_map/psum | solution.py:72
  290.8 1.0 copy-start.3
  291.9 255.7 %all-gather.5.cloned.1.call-start = ((), (), s32[]{:S(2)}) async-start(), calls=%async_computation.3 | async-start | bytes 1179648 | tf_op jit(solution)/shard_map/all_gather | solution.py:137
  369.6 1.7 copy-start.1
  371.5 1.0 copy-start.4
  372.5 21.7 %copy-start.5 = (f32[512,512]{1,0:T(8,128)S(1)}, f32[512,512]{1,0:T(8,128)}, u32[]{:S(2)}) copy-start(f32[512,512]{1,0:T(8,128)} %copy-done.4) | copy-start | bytes 3145732
  508.4 39.2 %copy-start.9 = (bf16[128,512]{0,1:T(8,128)(2,1)S(1)}, bf16[128,512]{0,1:T(8,128)(2,1)}, u32[]{:S(2)}) copy-start(bf16[128,512]{0,1:T(8,128)(2,1)} %fusion.17) | copy-start | bytes 393220
Sparse Core Ops, SparseCore 0:
  20.7 79.4 all-reduce.3
  249.8 38.9 all-gather.2
  292.3 77.2 all-reduce.5
  508.5 38.9 all-gather.4
where the time goes:
time: 567 us; the launch traced here: 557 us
  other arithmetic  251 us (44%)
  waiting for transfers between devices  241 us (43%)
  local copies, waits for them, and re-layouts  28 us (5%)
  between operations  19.6 us (3%)
  matrix products  12.5 us (2%)
    another operation x29, other arithmetic, on_device(): jnp.linalg.cholesky(diag_block)  158 us
    psum x2, waiting for transfers between devices, collect(): result = lax.psum(padded, 'blk')  157 us
    another operation x5, other arithmetic, own_rows(): lax.linalg.triangular_solve(diag_factor, panel_part, left_side=False, low...  90.8 us
    all_gather x2, waiting for transfers between devices, on_device(): lax.all_gather(lowered, 'blk', axis=0, tiled=True)  78.2 us
    another operation x27, local copies, waits for them, and re-layouts, own_rows(): lax.linalg.triangular_solve(diag_factor, panel_part, left_side=False, low...  16.5 us
  transfers between devices with their start and end apart: 5, of which 5 were waited for; matrix products, arithmetic and copies ran while one was open for 0% of the time, Pallas kernels for 0%

commit v1 on v0

--- a/solution.py
+++ b/solution.py
@@ -8,6 +8,14 @@
 COL_BLOCKS = 1
 TILE_WIDTH = 64
 HIGHEST = lax.Precision.HIGHEST
+
+
+def add_in_pairs(block, name):
+    count, total = (lax.axis_size(name), block)
+    for reach in [1 << k for k in range(count.bit_length() - 1)]:
+        route = [(i, i ^ reach) for i in range(count)]
+        total = total + lax.ppermute(total, name, route)
+    return total
 
 
 def from_behind(shard, axis, by):
@@ -69,7 +77,7 @@
     padded = lax.dynamic_update_slice(
         padded, jnp.where(is_owner, stacked, 0.0), (0, column_start, 0)
     )
-    result = lax.psum(padded, "blk")
+    result = add_in_pairs(padded, "blk")
     return result
 
 

time: 567 us -> 591 us (1.042)
  waiting for transfers between devices: 241 us -> 266 us
  starting transfers between devices: 4.19 us -> 13.6 us
    ppermute x0 -> x6, waiting for transfers between devices: none -> 180 us  [add_in_pairs(): total = total + lax.ppermute(total, name, route)]
    psum x2 -> x0, waiting for transfers between devices: 157 us -> none  [collect(): result = lax.psum(padded, 'blk')]
    another operation x5, other arithmetic: 90.8 us -> 79 us  [own_rows(): lax.linalg.triangular_solve(diag_factor, panel_part, left_side=False, low...]
    ppermute x0 -> x6, starting transfers between devices: none -> 9.49 us  [add_in_pairs(): total = total + lax.ppermute(total, name, route)]
  transfers between devices with their start and end apart: 5 -> 9, of which waited for: 5 -> 9; matrix products, arithmetic and copies ran while one was open for 0% -> 0% of each run, Pallas kernels for 0% -> 0%
where the time goes in v1:
time: 591 us; the launch traced here: 582 us
  waiting for transfers between devices  266 us (45%)
  other arithmetic  246 us (42%)
  local copies, waits for them, and re-layouts  24.4 us (4%)
  between operations  19.3 us (3%)
  starting transfers between devices  13.6 us (2%)
  matrix products  12.5 us (2%)
    ppermute x6, waiting for transfers between devices, add_in_pairs(): total = total + lax.ppermute(total, name, route)  180 us
    another operation x29, other arithmetic, on_device(): jnp.linalg.cholesky(diag_block)  159 us
    all_gather x2, waiting for transfers between devices, on_device(): lax.all_gather(lowered, 'blk', axis=0, tiled=True)  80 us
    another operation x5, other arithmetic, own_rows(): lax.linalg.triangular_solve(diag_factor, panel_part, left_side=False, low...  79 us
    another operation x27, local copies, waits for them, and re-layouts, own_rows(): lax.linalg.triangular_solve(diag_factor, panel_part, left_side=False, low...  16.5 us
  transfers between devices with their start and end apart: 9, of which 9 were waited for; matrix products, arithmetic and copies ran while one was open for 0% of the time, Pallas kernels for 0%

profile of v1, /device:TPU:0, one launch (start us, length us, event | category | flops | bytes accessed | tf_op | source)
XLA Modules:
  0.0 581.9 jit_solution(14537322844098712659)
XLA Ops:
  6.5 4.1 collective-permute-start
  11.5 5.7 collective-permute-done
  19.6 1.6 collective-permute-start.1
  21.2 22.8 %collective-permute-done.1 = f32[1,512,512]{1,2,0:T(8,128)S(1)} collective-permute-done((f32[1,512,512]{1,2,0:T(8,128)S(1)}, f32[1,512,512]{1,2,0:T(8,128)S(1)}, u32[]{:S(2)}, u32[]{:S(2)}) %collective-permute-start.1) | collective-permute-done | bytes 1048608 | tf_op jit(solution)/shard_map/ppermute | solution.py:17
  44.0 1.6 collective-permute-start.2
  45.7 22.5 %collective-permute-done.2 = f32[1,512,512]{1,2,0:T(8,128)S(1)} collective-permute-done((f32[1,512,512]{1,2,0:T(8,128)S(1)}, f32[1,512,512]{1,2,0:T(8,128)S(1)}, u32[]{:S(2)}, u32[]{:S(2)}) %collective-permute-start.2) | collective-permute-done | bytes 1048608 | tf_op jit(solution)/shard_map/ppermute | solution.py:17
  68.4 3.3 collective-permute-start.3
  71.8 44.4 %collective-permute-done.3 = f32[1,512,512]{1,2,0:T(8,128)} collective-permute-done((f32[1,512,512]{1,2,0:T(8,128)S(1)}, f32[1,512,512]{1,2,0:T(8,128)}, u32[]{:S(2)}, u32[]{:S(2)}) %collective-permute-start.3) | collective-permute-done | bytes 1048608 | tf_op jit(solution)/shard_map/ppermute | solution.py:17
  116.2 1.4 add_bitcast_fusion.1
  117.6 1.4 copy.13
  119.0 1.9 fusion.6
  120.9 11.7 %cholesky.286 = f32[128,128]{1,0:T(8,128)S(1)} custom-call(f32[128,128]{1,0:T(8,128)S(1)} %cholesky.426), custom_call_target="Cholesky" | custom-call | tf_op jit(solution)/shard_map/jit(cholesky)/cholesky | solution.py:141
  132.8 9.8 %custom-call.27 = f32[1,128,128]{1,2,0:T(8,128)S(1)} custom-call(f32[1,128,128]{2,1,0:T(8,128)S(1)} %get-tuple-element.73), custom_call_target="InvertDiagBlocksLowerTriangular" | custom-call | tf_op jit(solution)/shard_map/jit(cholesky)/cholesky | solution.py:141
  143.3 12.1 %cholesky.305 = f32[128,128]{1,0:T(8,128)S(1)} custom-call(f32[128,128]{1,0:T(8,128)S(1)} %cholesky.430), custom_call_target="Cholesky" | custom-call | tf_op jit(solution)/shard_map/jit(cholesky)/cholesky | solution.py:141
  155.4 9.8 %custom-call.28 = f32[1,128,128]{1,2,0:T(8,128)S(1)} custom-call(f32[1,128,128]{2,1,0:T(8,128)S(1)} %get-tuple-element.70), custom_call_target="InvertDiagBlocksLowerTriangular" | custom-call | tf_op jit(solution)/shard_map/jit(cholesky)/cholesky | solution.py:141
  165.9 11.7 %cholesky.326 = f32[128,128]{1,0:T(8,128)S(1)} custom-call(f32[128,128]{1,0:T(8,128)S(1)} %cholesky.435), custom_call_target="Cholesky" | custom-call | tf_op jit(solution)/shard_map/jit(cholesky)/cholesky | solution.py:141
  178.4 9.8 %custom-call.29 = f32[1,128,128]{1,2,0:T(8,128)S(1)} custom-call(f32[1,128,128]{2,1,0:T(8,128)S(1)} %get-tuple-element.67), custom_call_target="InvertDiagBlocksLowerTriangular" | custom-call | tf_op jit(solution)/shard_map/jit(cholesky)/cholesky | solution.py:141
  188.8 11.9 %cholesky.343 = f32[128,128]{1,0:T(8,128)S(1)} custom-call(f32[128,128]{1,0:T(8,128)S(1)} %slice_subtract_fusion.5), custom_call_target="Cholesky" | custom-call | tf_op jit(solution)/shard_map/jit(cholesky)/cholesky | solution.py:141
  204.8 8.1 %while.4 = (s32[]{:T(128)}, f32[512,512]{1,0:T(8,128)S(1)}, s32[4,2]{0,1:T(2,128)S(1)}, f32[4,128,128]{2,1,0:T(8,128)S(1)}, s32[]{:T(128)}) while((s32[]{:T(128)}, f32[512,512]{1,0:T(8,128)S(1)}, s32[4,2]{0,1:T(2,128)S(1)}, f32[4,128,128]{2,1,0:T(8,128)S(1)}, s32[]{:T(128)}) %tuple.61), condition=%wide.while_cond, body=%wide.while_body.sunk | while | flops 2 | bytes 131181 | solution.py:85
  205.5 1.3 bitcast_dynamic-update-slice_fusion.4
  207.5 1.3 bitcast_dynamic-update-slice_fusion.4
  209.6 1.3 bitcast_dynamic-update-slice_fusion.4
  211.6 1.3 bitcast_dynamic-update-slice_fusion.4
  213.0 39.3 %custom-call.30 = f32[4,128,128]{1,2,0:T(8,128)S(1)} custom-call(f32[4,128,128]{2,1,0:T(8,128)S(1)} %get-tuple-element.22), custom_call_target="InvertDiagBlocksLowerTriangular" | custom-call | tf_op jit(solution)/shard_map/triangular_solve/custom-call.3 | solution.py:85
  256.1 40.7 %all-gather.3.cloned.1.call-done = bf16[1024,512]{0,1:T(8,128)(2,1)} async-done(((bf16[128,512]{0,1:T(8,128)(2,1)}), bf16[1024,512]{0,1:T(8,128)(2,1)}) %all-gather.3.cloned.1.call-update) | async-done | bytes 1048592 | tf_op jit(solution)/shard_map/all_gather | solution.py:145
  296.8 1.6 fusion
  298.8 1.1 collective-permute-start.4
  299.9 23.1 %collective-permute-done.4 = f32[1,512,512]{1,2,0:T(8,128)S(1)} collective-permute-done((f32[1,512,512]{1,2,0:T(8,128)S(1)}, f32[1,512,512]{1,2,0:T(8,128)S(1)}, u32[]{:S(2)}, u32[]{:S(2)}) %collective-permute-start.4) | collective-permute-done | bytes 1048608 | tf_op jit(solution)/shard_map/ppermute | solution.py:17
  323.2 23.3 %collective-permute-done.5 = f32[1,512,512]{1,2,0:T(8,128)S(1)} collective-permute-done((f32[1,512,512]{1,2,0:T(8,128)S(1)}, f32[1,512,512]{1,2,0:T(8,128)S(1)}, u32[]{:S(2)}, u32[]{:S(2)}) %collective-permute-start.5) | collective-permute-done | bytes 1048608 | tf_op jit(solution)/shard_map/ppermute | solution.py:17
  346.7 1.7 collective-permute-start.6
  348.5 44.1 %collective-permute-done.6 = f32[1,512,512]{1,2,0:T(8,128)S(1)} collective-permute-done((f32[1,512,512]{1,2,0:T(8,128)S(1)}, f32[1,512,512]{1,2,0:T(8,128)S(1)}, u32[]{:S(2)}, u32[]{:S(2)}) %collective-permute-start.6) | collective-permute-done | bytes 1048608 | tf_op jit(solution)/shard_map/ppermute | solution.py:17
  393.8 1.3 copy.16
  395.2 1.9 fusion.5
  397.1 11.7 %cholesky.358 = f32[128,128]{1,0:T(8,128)S(1)} custom-call(f32[128,128]{1,0:T(8,128)S(1)} %cholesky.439), custom_call_target="Cholesky" | custom-call | tf_op jit(solution)/shard_map/jit(cholesky)/cholesky | solution.py:141
  409.0 9.8 %custom-call.31 = f32[1,128,128]{1,2,0:T(8,128)S(1)} custom-call(f32[1,128,128]{2,1,0:T(8,128)S(1)} %get-tuple-element.63), custom_call_target="InvertDiagBlocksLowerTriangular" | custom-call | tf_op jit(solution)/shard_map/jit(cholesky)/cholesky | solution.py:141
  419.4 12.1 %cholesky.377 = f32[128,128]{1,0:T(8,128)S(1)} custom-call(f32[128,128]{1,0:T(8,128)S(1)} %cholesky.443), custom_call_target="Cholesky" | custom-call | tf_op jit(solution)/shard_map/jit(cholesky)/cholesky | solution.py:141
  432.9 9.8 %custom-call.32 = f32[1,128,128]{1,2,0:T(8,128)S(1)} custom-call(f32[1,128,128]{2,1,0:T(8,128)S(1)} %get-tuple-element.60), custom_call_target="InvertDiagBlocksLowerTriangular" | custom-call | tf_op jit(solution)/shard_map/jit(cholesky)/cholesky | solution.py:141
  443.4 11.7 %cholesky.398 = f32[128,128]{1,0:T(8,128)S(1)} custom-call(f32[128,128]{1,0:T(8,128)S(1)} %cholesky.448), custom_call_target="Cholesky" | custom-call | tf_op jit(solution)/shard_map/jit(cholesky)/cholesky | solution.py:141
  455.8 9.8 %custom-call.33 = f32[1,128,128]{1,2,0:T(8,128)S(1)} custom-call(f32[1,128,128]{2,1,0:T(8,128)S(1)} %get-tuple-element.57), custom_call_target="InvertDiagBlocksLowerTriangular" | custom-call | tf_op jit(solution)/shard_map/jit(cholesky)/cholesky | solution.py:141
  466.2 11.9 %cholesky.415 = f32[128,128]{1,0:T(8,128)S(1)} custom-call(f32[128,128]{1,0:T(8,128)S(1)} %slice_subtract_fusion.4), custom_call_target="Cholesky" | custom-call | tf_op jit(solution)/shard_map/jit(cholesky)/cholesky | solution.py:141
  481.5 8.5 %while.5 = (s32[]{:T(128)}, f32[512,512]{1,0:T(8,128)S(1)}, s32[4,2]{0,1:T(2,128)S(1)}, f32[4,128,128]{2,1,0:T(8,128)S(1)}, s32[]{:T(128)}) while((s32[]{:T(128)}, f32[512,512]{1,0:T(8,128)S(1)}, s32[4,2]{0,1:T(2,128)S(1)}, f32[4,128,128]{2,1,0:T(8,128)S(1)}, s32[]{:T(128)}) %tuple.71), condition=%wide.while_cond.clone, body=%wide.while_body.clone.sunk | while | flops 2 | bytes 131181 | solution.py:85
  482.2 1.4 bitcast_dynamic-update-slice_fusion.5
  484.3 1.4 bitcast_dynamic-update-slice_fusion.5
  486.5 1.4 bitcast_dynamic-update-slice_fusion.5
  488.6 1.4 bitcast_dynamic-update-slice_fusion.5
  490.0 39.3 %custom-call.34 = f32[4,128,128]{1,2,0:T(8,128)S(1)} custom-call(f32[4,128,128]{2,1,0:T(8,128)S(1)} %get-tuple-element.23), custom_call_target="InvertDiagBlocksLowerTriangular" | custom-call | tf_op jit(solution)/shard_map/triangular_solve/custom-call.3 | solution.py:85
  533.1 39.3 %all-gather.5.cloned.1.call-done = bf16[1024,512]{0,1:T(8,128)(2,1)} async-done(((bf16[128,512]{0,1:T(8,128)(2,1)}), bf16[1024,512]{0,1:T(8,128)(2,1)}) %all-gather.5.cloned.1.call-update) | async-done | bytes 1048592 | tf_op jit(solution)/shard_map/all_gather | solution.py:145
  572.4 2.4 fusion.3
  (123 shorter events, 27.7 us)
Async XLA Ops:
  6.5 290.2 %all-gather.3.cloned.1.call-start = ((), (), s32[]{:S(2)}) async-start(), calls=%async_computation | async-start | bytes 1179648 | tf_op jit(solution)/shard_map/all_gather | solution.py:145
  6.5 10.6 %collective-permute-start = (f32[1,64,512]{2,1,0:T(8,128)}, f32[1,64,512]{2,1,0:T(8,128)S(1)}, u32[]{:S(2)}, u32[]{:S(2)}) collective-permute-start(f32[1,64,512]{2,1,0:T(8,128)} %param.9), channel_id=1, source_target_pairs={{0,4},{1,5},{2,6},{3,7},{4,0},{5,1},{6,2},{7,3},{8,12},{9,13},{10,... | collective-permute-start | bytes 393224 | tf_op jit(solution)/shard_map/ppermute | solution.py:23
  17.6 1.0 copy-start.3
  19.6 24.4 %collective-permute-start.1 = (f32[1,512,512]{1,2,0:T(8,128)S(1)}, f32[1,512,512]{1,2,0:T(8,128)S(1)}, u32[]{:S(2)}, u32[]{:S(2)}) collective-permute-start(f32[1,512,512]{1,2,0:T(8,128)S(1)} %constant_dynamic-update-slice_fusion.3), channel_id=1, source_target_pairs={{0,1},{1,0},{2,3},{3,2},{4,5},{5,4},{6,7},{7,6},{8,9},{9,8},{10,11... | collective-permute-start | bytes 3145736 | tf_op jit(solution)/shard_map/ppermute | solution.py:17
  44.0 24.1 %collective-permute-start.2 = (f32[1,512,512]{1,2,0:T(8,128)S(1)}, f32[1,512,512]{1,2,0:T(8,128)S(1)}, u32[]{:S(2)}, u32[]{:S(2)}) collective-permute-start(f32[1,512,512]{1,2,0:T(8,128)S(1)} %add_dynamic-update-slice_fusion.1), channel_id=1, source_target_pairs={{0,2},{1,3},{2,0},{3,1},{4,6},{5,7},{6,4},{7,5},{8,10},{9,11},{10,... | collective-permute-start | bytes 3145736 | tf_op jit(solution)/shard_map/ppermute | solution.py:17
  68.4 47.8 %collective-permute-start.3 = (f32[1,512,512]{1,2,0:T(8,128)S(1)}, f32[1,512,512]{1,2,0:T(8,128)}, u32[]{:S(2)}, u32[]{:S(2)}) collective-permute-start(f32[1,512,512]{1,2,0:T(8,128)S(1)} %add.213), channel_id=1, source_target_pairs={{0,4},{1,5},{2,6},{3,7},{4,0},{5,1},{6,2},{7,3},{8,12},{9,13},{10,... | collective-permute-start | bytes 3145736 | tf_op jit(solution)/shard_map/ppermute | solution.py:17
  256.0 40.8 %copy-start.1 = (bf16[128,512]{0,1:T(8,128)(2,1)S(1)}, bf16[128,512]{0,1:T(8,128)(2,1)}, u32[]{:S(2)}) copy-start(bf16[128,512]{0,1:T(8,128)(2,1)} %fusion.17) | copy-start | bytes 393220
  256.0 316.4 %all-gather.5.cloned.1.call-start = ((), (), s32[]{:S(2)}) async-start(), calls=%async_computation.1 | async-start | bytes 1179648 | tf_op jit(solution)/shard_map/all_gather | solution.py:145
  298.8 24.2 %collective-permute-start.4 = (f32[1,512,512]{1,2,0:T(8,128)S(1)}, f32[1,512,512]{1,2,0:T(8,128)S(1)}, u32[]{:S(2)}, u32[]{:S(2)}) collective-permute-start(f32[1,512,512]{1,2,0:T(8,128)S(1)} %constant_dynamic-update-slice_fusion.2), channel_id=1, source_target_pairs={{0,1},{1,0},{2,3},{3,2},{4,5},{5,4},{6,7},{7,6},{8,9},{9,8},{10,11... | collective-permute-start | bytes 3145736 | tf_op jit(solution)/shard_map/ppermute | solution.py:17
  323.1 23.4 %collective-permute-start.5 = (f32[1,512,512]{1,2,0:T(8,128)S(1)}, f32[1,512,512]{1,2,0:T(8,128)S(1)}, u32[]{:S(2)}, u32[]{:S(2)}) collective-permute-start(f32[1,512,512]{1,2,0:T(8,128)S(1)} %add_dynamic-update-slice_fusion), channel_id=1, source_target_pairs={{0,2},{1,3},{2,0},{3,1},{4,6},{5,7},{6,4},{7,5},{8,10},{9,11},{10,... | collective-permute-start | bytes 3145736 | tf_op jit(solution)/shard_map/ppermute | solution.py:17
  346.7 45.9 %collective-permute-start.6 = (f32[1,512,512]{1,2,0:T(8,128)S(1)}, f32[1,512,512]{1,2,0:T(8,128)S(1)}, u32[]{:S(2)}, u32[]{:S(2)}) collective-permute-start(f32[1,512,512]{1,2,0:T(8,128)S(1)} %add.217), channel_id=1, source_target_pairs={{0,4},{1,5},{2,6},{3,7},{4,0},{5,1},{6,2},{7,3},{8,12},{9,13},{10,... | collective-permute-start | bytes 3145736 | tf_op jit(solution)/shard_map/ppermute | solution.py:17
  392.6 1.0 copy-start
  533.0 39.4 %copy-start.2 = (bf16[128,512]{0,1:T(8,128)(2,1)S(1)}, bf16[128,512]{0,1:T(8,128)(2,1)}, u32[]{:S(2)}) copy-start(bf16[128,512]{0,1:T(8,128)(2,1)} %fusion.19) | copy-start | bytes 393220
Sparse Core Ops, SparseCore 0:
  256.1 40.5 all-gather.2
  533.2 39.1 all-gather.4
